TPU v7x, 32 devices: a whole 2x2x4 slice. The times are simulated.
32 devices in a mesh: owner: 4 (over x, core), rows: 8 (over z, y).
Axes of the slice: x: 2, y: 2, z: 4, core: 2. Of those that a mesh axis runs over, the one named last changes fastest.
Arguments:
- master_gate: float32 [64, 2048, 1408], P('owner', 'rows'), may hold values from -0.1875 to 0.1875
- master_up: float32 [64, 2048, 1408], P('owner', 'rows'), may hold values from -0.1875 to 0.1875
- router_weight: float32 [2048, 64], P('rows', 'owner'), may hold values from -0.125 to 0.125
- router_gain: float32 [2048], P('rows'), may hold values from 0.25 to 1.75
Outputs:
- final_gate: bfloat16 [64, 2048, 1408], P('owner', None, 'rows')
- final_up: bfloat16 [64, 2048, 1408], P('owner', None, 'rows')
- scale_gate: float32 [64, 1408], P('owner', 'rows')
- scale_up: float32 [64, 1408], P('owner', 'rows')
- serve_router: bfloat16 [2048, 64], replicated
All inputs are finite; a program needn't handle non-finite values. Where the computation divides by a largest or mean magnitude, that divisor is 1e-20 or more.
Results may differ from a plain program's by a relative error of at most 0.001.
Values may be sent and summed in bfloat16 or wider, within the bound.
A program may use at most 192 MiB of HBM per device.

v0:
```python
import jax
import jax.numpy as jnp
from jax import lax
from jax.sharding import PartitionSpec as P


def shards(master_gate, master_up, router_weight, router_gain):
    scale_gate, scale_up = lax.pmax(
        (jnp.max(jnp.abs(master_gate), axis=1), jnp.max(jnp.abs(master_up), axis=1)), "rows"
    )
    narrow_gate, narrow_up = (
        (master_gate / jnp.expand_dims(scale_gate, 1)).astype(jnp.bfloat16),
        (master_up / jnp.expand_dims(scale_up, 1)).astype(jnp.bfloat16),
    )
    final_gate, final_up = (
        lax.all_to_all(narrow_gate, "rows", split_axis=2, concat_axis=1, tiled=True),
        lax.all_to_all(narrow_up, "rows", split_axis=2, concat_axis=1, tiled=True),
    )
    scale_gate = lax.dynamic_slice_in_dim(
        scale_gate, lax.axis_index("rows") * final_gate.shape[2], final_gate.shape[2], axis=1
    )
    scale_up = lax.dynamic_slice_in_dim(
        scale_up, lax.axis_index("rows") * final_up.shape[2], final_up.shape[2], axis=1
    )
    part_router = (router_weight * router_gain[:, None]).astype(jnp.bfloat16)
    row_router = lax.all_gather(part_router, "rows", axis=0, tiled=True)
    serve_router = lax.all_gather(row_router, "owner", axis=1, tiled=True)
    return (final_gate, final_up, scale_gate, scale_up, serve_router)


def solution(mesh):
    return jax.shard_map(
        shards,
        mesh=mesh,
        in_specs=(
            P("owner", "rows", None),
            P("owner", "rows", None),
            P("rows", "owner"),
            P("rows"),
        ),
        out_specs=(
            P("owner", None, "rows"),
            P("owner", None, "rows"),
            P("owner", "rows"),
            P("owner", "rows"),
            P(),
        ),
        check_vma=False,
    )
```

profile of v0, /device:TPU:0, one launch (start us, length us, event | category | flops | bytes accessed | tf_op | source)
XLA Modules:
  0.0 714.9 jit_solution(11512561346431727942)
XLA Ops:
  7.2 0.0 all-reduce.3.cloned.1.call-start
  7.2 0.0 copy-start
  7.2 9.7 %abs_reduce_fusion = f32[16,1408]{1,0:T(8,128)} fusion(f32[16,256,1408]{2,1,0:T(8,128)} %param.5), kind=kLoop, calls=%fused_computation.1 | loop fusion | flops 11511808 | bytes 23158784 | tf_op jit(solution)/shard_map/reduce_max | solution.py:9
  16.9 4.5 copy-done
  21.4 2.4 abs_reduce_fusion.1
  23.8 0.0 all-reduce.3.cloned.1.call-update
  23.8 23.7 %copy.18 = f32[16,256,1408]{1,0,2:T(8,128)} copy(f32[16,256,1408]{2,1,0:T(8,128)} %param.4) | data formatting | bytes 46137344 | tf_op args[0]
  47.5 50.1 %all-reduce.3.cloned.1.call-done = (f32[16,1408]{1,0:T(8,128)}, f32[16,1408]{1,0:T(8,128)}) async-done(((f32[16,1408]{1,0:T(8,128)}, f32[16,1408]{1,0:T(8,128)}), (f32[16,1408]{1,0:T(8,128)}, f32[16,1408]{1,0:T(8,128)})) %all-reduce.3.cloned.1.call-update) | async-done | bytes 180240 | tf_op jit(solution)/shard_map/pmax | solution.py:8
  97.6 1.1 copy.17
  98.8 14.2 %divide_convert_fusion.1 = bf16[16,256,1408]{1,0,2:T(8,128)(2,1)} fusion(f32[16,256,1408]{1,0,2:T(8,128)} %copy.18, f32[16,1408]{0,1:T(8,128)S(1)} %copy.17), kind=kLoop, calls=%fused_computation.2 | loop fusion | flops 11534336 | bytes 34693120 | tf_op jit(solution)/shard_map/convert_element_type | solution.py:12
  113.0 5.2 all-to-all-start
  118.3 23.7 %copy.22 = f32[16,256,1408]{1,0,2:T(8,128)} copy(f32[16,256,1408]{2,1,0:T(8,128)} %param.5) | data formatting | bytes 46137344 | tf_op args[1]
  142.0 0.3 copy.21
  142.3 14.2 %divide_convert_fusion = bf16[16,256,1408]{1,0,2:T(8,128)(2,1)} fusion(f32[16,256,1408]{1,0,2:T(8,128)} %copy.22, f32[16,1408]{0,1:T(8,128)S(1)} %copy.21), kind=kLoop, calls=%fused_computation | loop fusion | flops 11534336 | bytes 34693120 | tf_op jit(solution)/shard_map/convert_element_type | solution.py:13
  156.5 210.6 %all-to-all-done = bf16[16,256,1408]{1,0,2:T(8,128)(2,1)} async-done(((bf16[16,256,1408]{1,0,2:T(8,128)(2,1)}), bf16[16,256,1408]{1,0,2:T(8,128)(2,1)}, u32[]{:S(2)}, u32[]{:S(2)}) %all-to-all-start) | async-done | bytes 11534368 | tf_op jit(solution)/shard_map/all_to_all | solution.py:16
  367.1 5.3 all-to-all-start.1
  372.4 269.1 %all_gather.6 = bf16[2048,16]{0,1:T(8,128)(2,1)S(1)} all-gather(bf16[256,16]{0,1:T(8,128)(2,1)S(1)} %multiply_convert_fusion), channel_id=1, replica_groups=mesh['owner'=4,'rows'=8] {'rows'}, dimensions={0}, use_global_device_ids=true | all-gather | bytes 73728 | tf_op jit(solution)/shard_map/all_gather | solution.py:26
  641.5 5.8 all_gather.7
  647.3 1.4 constant_dynamic-slice_fusion
  648.7 11.3 %copy.20 = bf16[16,8,256,176]{2,1,3,0:T(8,128)(2,1)} copy(bf16[16,8,256,176]{2,0,3,1:T(8,128)(2,1)} %bitcast.2) | data formatting | bytes 23068672 | tf_op jit(solution)/shard_map/all_to_all | solution.py:16
  660.0 18.0 %all_to_all.29 = bf16[16,2048,176]{1,2,0:T(8,128)(2,1)} reshape(bf16[16,8,256,176]{2,1,3,0:T(8,128)(2,1)} %copy.20) | data formatting | bytes 23068672 | tf_op jit(solution)/shard_map/all_to_all | solution.py:16
  678.0 11.4 %copy.24 = bf16[16,8,256,176]{2,1,3,0:T(8,128)(2,1)} copy(bf16[16,8,256,176]{2,0,3,1:T(8,128)(2,1)} %bitcast.5) | data formatting | bytes 23068672 | tf_op jit(solution)/shard_map/all_to_all | solution.py:17
  689.4 18.0 %all_to_all.33 = bf16[16,2048,176]{1,2,0:T(8,128)(2,1)} reshape(bf16[16,8,256,176]{2,1,3,0:T(8,128)(2,1)} %copy.24) | data formatting | bytes 23068672 | tf_op jit(solution)/shard_map/all_to_all | solution.py:17
  707.3 0.7 copy.30
  (8 shorter events, 0.0 us)
Async XLA Ops:
  7.2 90.5 %all-reduce.3.cloned.1.call-start = ((), (), s32[]{:S(2)}) async-start(), calls=%async_computation.2 | async-start | bytes 360448 | tf_op jit(solution)/shard_map/pmax | solution.py:8
  7.2 14.2 %copy-start = (f32[16,256,1408]{2,1,0:T(8,128)S(1)}, f32[16,256,1408]{2,1,0:T(8,128)}, u32[]{:S(2)}) copy-start(f32[16,256,1408]{2,1,0:T(8,128)} %param.4) | copy-start | bytes 69206016
  113.0 254.0 %all-to-all-start = ((bf16[16,256,1408]{1,0,2:T(8,128)(2,1)}), bf16[16,256,1408]{1,0,2:T(8,128)(2,1)}, u32[]{:S(2)}, u32[]{:S(2)}) async-start(bf16[16,256,1408]{1,0,2:T(8,128)(2,1)} %divide_convert_fusion.1), calls=%async_computation | async-start | bytes 23068672 | tf_op jit(solution)/shard_map/all_to_all | solution.py:16
  118.3 23.7 %copy-start.1 = (f32[16,1408]{1,0:T(8,128)S(1)}, f32[16,1408]{1,0:T(8,128)}, u32[]{:S(2)}) copy-start(f32[16,1408]{1,0:T(8,128)} %get-tuple-element.6) | copy-start | bytes 270340
  142.3 230.1 %copy-start.2 = (f32[256,16]{0,1:T(8,128)S(1)}, f32[256,16]{0,1:T(8,128)}, u32[]{:S(2)}) copy-start(f32[256,16]{0,1:T(8,128)} %param.6) | copy-start | bytes 49156
  142.3 230.1 %copy-start.3 = (f32[256]{0:T(256)S(1)}, f32[256]{0:T(256)}, u32[]{:S(2)}) copy-start(f32[256]{0:T(256)} %param.7) | copy-start | bytes 3076
  367.1 310.9 %all-to-all-start.1 = ((bf16[16,256,1408]{1,0,2:T(8,128)(2,1)}), bf16[16,256,1408]{1,0,2:T(8,128)(2,1)}, u32[]{:S(2)}, u32[]{:S(2)}) async-start(bf16[16,256,1408]{1,0,2:T(8,128)(2,1)} %divide_convert_fusion), calls=%async_computation.1 | async-start | bytes 23068672 | tf_op jit(solution)/shard_map/all_to_all | solution.py:17
Sparse Core Ops, SparseCore 0:
  24.0 73.6 all-reduce.2
where the time goes:
time: 717 us; the launch traced here: 715 us
  blocking collectives  275 us (38%)
  waiting for transfers between devices  261 us (36%)
  local copies, waits for them, and re-layouts  114 us (16%)
  other arithmetic  40.5 us (6%)
  between operations  14.1 us (2%)
  starting transfers between devices  10.5 us (1%)
    all_gather x1, blocking collectives, shards(): row_router = lax.all_gather(part_router, 'rows', axis=0, tiled=True)  269 us
    all_to_all x1, waiting for transfers between devices, shards(): lax.all_to_all(narrow_gate, 'rows', split_axis=2, concat_axis=1, tiled=True)  211 us
    unnamed x11, local copies, waits for them, and re-layouts  52.6 us
    pmax x1, waiting for transfers between devices, shards(): lax.pmax((jnp.max(jnp.abs(master_gate), axis=1), jnp.max(jnp.abs(master_u...  50.1 us
    all_to_all x2, local copies, waits for them, and re-layouts, shards(): lax.all_to_all(narrow_up, 'rows', split_axis=2, concat_axis=1, tiled=True)  29.3 us
    all_to_all x2, local copies, waits for them, and re-layouts, shards(): lax.all_to_all(narrow_gate, 'rows', split_axis=2, concat_axis=1, tiled=True)  29.3 us
  transfers between devices with their start and end apart: 3, of which 2 were waited for; matrix products, arithmetic and copies ran while one was open for 10% of the time, Pallas kernels for 0%

commit v1 on v0

--- a/solution.py
+++ b/solution.py
@@ -13,7 +13,12 @@
         (master_up / jnp.expand_dims(scale_up, 1)).astype(jnp.bfloat16),
     )
     final_gate, final_up = (
-        lax.all_to_all(narrow_gate, "rows", split_axis=2, concat_axis=1, tiled=True),
+        jnp.concatenate(
+            lax.all_to_all(
+                jnp.stack(jnp.split(narrow_gate, lax.axis_size("rows"), axis=2)), "rows", 0, 0
+            ),
+            axis=1,
+        ),
         lax.all_to_all(narrow_up, "rows", split_axis=2, concat_axis=1, tiled=True),
     )
     scale_gate = lax.dynamic_slice_in_dim(

time: 717 us -> 701 us (0.978)
  local copies, waits for them, and re-layouts: 114 us -> 103 us
    all_to_all x2 -> x0, local copies, waits for them, and re-layouts: 29.3 us -> none  [shards(): lax.all_to_all(narrow_gate, 'rows', split_axis=2, concat_axis=1, tiled=True)]
    reshape x0 -> x1, local copies, waits for them, and re-layouts: none -> 10 us  [shards(): jnp.concatenate(lax.all_to_all(jnp.stack(jnp.split(narrow_gate, lax.axis_...]
    unnamed x11 -> x18, local copies, waits for them, and re-layouts: 52.6 us -> 60.7 us
where the time goes in v1:
time: 701 us; the launch traced here: 700 us
  blocking collectives  275 us (39%)
  waiting for transfers between devices  261 us (37%)
  local copies, waits for them, and re-layouts  103 us (15%)
  other arithmetic  36.1 us (5%)
  between operations  14.1 us (2%)
  starting transfers between devices  10.5 us (1%)
    all_gather x1, blocking collectives, shards(): row_router = lax.all_gather(part_router, 'rows', axis=0, tiled=True)  269 us
    all_to_all x1, waiting for transfers between devices, shards(): lax.all_to_all(jnp.stack(jnp.split(narrow_gate, lax.axis_size('rows'), ax...  211 us
    unnamed x18, local copies, waits for them, and re-layouts  60.7 us
    pmax x1, waiting for transfers between devices, shards(): lax.pmax((jnp.max(jnp.abs(master_gate), axis=1), jnp.max(jnp.abs(master_u...  50.4 us
    all_to_all x2, local copies, waits for them, and re-layouts, shards(): lax.all_to_all(narrow_up, 'rows', split_axis=2, concat_axis=1, tiled=True)  29.3 us
    convert_element_type x1, other arithmetic, shards(): (master_up / jnp.expand_dims(scale_up, 1)).astype(jnp.bfloat16)  14.2 us
  transfers between devices with their start and end apart: 3, of which 2 were waited for; matrix products, arithmetic and copies ran while one was open for 10% of the time, Pallas kernels for 0%

profile of v1, /device:TPU:0, one launch (start us, length us, event | category | flops | bytes accessed | tf_op | source)
XLA Modules:
  0.0 699.6 jit_solution(4645393011724028412)
XLA Ops:
  7.2 9.7 %abs_reduce_fusion = f32[16,1408]{1,0:T(8,128)} fusion(f32[16,256,1408]{2,1,0:T(8,128)} %param.5), kind=kLoop, calls=%fused_computation.1 | loop fusion | flops 11511808 | bytes 23158784 | tf_op jit(solution)/shard_map/reduce_max | solution.py:9
  16.9 4.5 copy-done
  21.4 2.4 abs_reduce_fusion.1
  23.8 23.3 %copy.21 = f32[16,256,1408]{1,2,0:T(8,128)} copy(f32[16,256,1408]{2,1,0:T(8,128)} %param.4) | data formatting | bytes 46137344 | tf_op args[0]
  47.2 50.4 %all-reduce.3.cloned.1.call-done = (f32[16,1408]{1,0:T(8,128)}, f32[16,1408]{1,0:T(8,128)}) async-done(((f32[16,1408]{1,0:T(8,128)}, f32[16,1408]{1,0:T(8,128)}), (f32[16,1408]{1,0:T(8,128)}, f32[16,1408]{1,0:T(8,128)})) %all-reduce.3.cloned.1.call-update) | async-done | bytes 180240 | tf_op jit(solution)/shard_map/pmax | solution.py:8
  97.6 9.8 %divide_convert_fusion.1 = bf16[16,256,1408]{1,2,0:T(8,128)(2,1)S(1)} fusion(f32[16,256,1408]{1,2,0:T(8,128)} %copy.21, f32[16,1408]{1,0:T(8,128)} %get-tuple-element.5), kind=kLoop, calls=%fused_computation.2 | loop fusion | flops 11534336 | bytes 34693120 | tf_op jit(solution)/shard_map/convert_element_type | solution.py:12
  107.5 1.2 fusion.7
  108.7 1.2 fusion.6
  109.8 1.2 fusion.5
  111.0 1.2 fusion.4
  112.2 1.2 fusion.3
  114.6 1.2 fusion.1
  115.8 1.2 fusion
  117.0 5.2 all-to-all-start
  122.3 23.7 %copy.24 = f32[16,256,1408]{1,0,2:T(8,128)} copy(f32[16,256,1408]{2,1,0:T(8,128)} %param.5) | data formatting | bytes 46137344 | tf_op args[1]
  146.3 14.2 %divide_convert_fusion = bf16[16,256,1408]{1,0,2:T(8,128)(2,1)} fusion(f32[16,256,1408]{1,0,2:T(8,128)} %copy.24, f32[16,1408]{0,1:T(8,128)S(1)} %copy.23), kind=kLoop, calls=%fused_computation | loop fusion | flops 11534336 | bytes 34693120 | tf_op jit(solution)/shard_map/convert_element_type | solution.py:13
  160.5 210.6 %all-to-all-done = bf16[8,16,256,176]{2,3,1,0:T(8,128)(2,1)} async-done(((bf16[8,16,256,176]{2,3,1,0:T(8,128)(2,1)}), bf16[8,16,256,176]{2,3,1,0:T(8,128)(2,1)}, u32[]{:S(2)}, u32[]{:S(2)}) %all-to-all-start) | async-done | bytes 11534368 | tf_op jit(solution)/shard_map/all_to_all | solution.py:17
  371.1 5.3 all-to-all-start.1
  376.4 269.1 %all_gather.6 = bf16[2048,16]{0,1:T(8,128)(2,1)S(1)} all-gather(bf16[256,16]{0,1:T(8,128)(2,1)S(1)} %multiply_convert_fusion), channel_id=1, replica_groups=mesh['owner'=4,'rows'=8] {'rows'}, dimensions={0}, use_global_device_ids=true | all-gather | bytes 73728 | tf_op jit(solution)/shard_map/all_gather | solution.py:31
  645.5 5.8 all_gather.7
  651.3 1.4 constant_dynamic-slice_fusion
  652.7 10.0 %copy.28 = bf16[8,16,22,8,256]{4,3,0,2,1:T(8,128)(2,1)} copy(bf16[8,16,22,8,256]{4,3,2,1,0:T(8,128)(2,1)} %bitcast.12) | data formatting | bytes 23068672 | tf_op jit(solution)/shard_map/reshape | solution.py:16
  662.7 11.4 %copy.26 = bf16[16,8,256,176]{2,1,3,0:T(8,128)(2,1)} copy(bf16[16,8,256,176]{2,0,3,1:T(8,128)(2,1)} %bitcast.11) | data formatting | bytes 23068672 | tf_op jit(solution)/shard_map/all_to_all | solution.py:22
  674.1 18.0 %all_to_all.20 = bf16[16,2048,176]{1,2,0:T(8,128)(2,1)} reshape(bf16[16,8,256,176]{2,1,3,0:T(8,128)(2,1)} %copy.26) | data formatting | bytes 23068672 | tf_op jit(solution)/shard_map/all_to_all | solution.py:22
  (14 shorter events, 2.2 us)
Async XLA Ops:
  7.2 90.5 %all-reduce.3.cloned.1.call-start = ((), (), s32[]{:S(2)}) async-start(), calls=%async_computation.2 | async-start | bytes 360448 | tf_op jit(solution)/shard_map/pmax | solution.py:8
  7.2 14.2 %copy-start = (f32[16,256,1408]{2,1,0:T(8,128)S(1)}, f32[16,256,1408]{2,1,0:T(8,128)}, u32[]{:S(2)}) copy-start(f32[16,256,1408]{2,1,0:T(8,128)} %param.4) | copy-start | bytes 69206016
  117.0 254.0 %all-to-all-start = ((bf16[8,16,256,176]{2,3,1,0:T(8,128)(2,1)}), bf16[8,16,256,176]{2,3,1,0:T(8,128)(2,1)}, u32[]{:S(2)}, u32[]{:S(2)}) async-start(bf16[8,16,256,176]{2,3,1,0:T(8,128)(2,1)} %fusion), calls=%async_computation | async-start | bytes 23068672 | tf_op jit(solution)/shard_map/all_to_all | solution.py:17
  122.3 23.7 %copy-start.1 = (f32[16,1408]{1,0:T(8,128)S(1)}, f32[16,1408]{1,0:T(8,128)}, u32[]{:S(2)}) copy-start(f32[16,1408]{1,0:T(8,128)} %get-tuple-element.6) | copy-start | bytes 270340
  160.5 215.9 %copy-start.2 = (f32[256,16]{0,1:T(8,128)S(1)}, f32[256,16]{0,1:T(8,128)}, u32[]{:S(2)}) copy-start(f32[256,16]{0,1:T(8,128)} %param.6) | copy-start | bytes 49156
  160.5 215.9 %copy-start.3 = (f32[256]{0:T(256)S(1)}, f32[256]{0:T(256)}, u32[]{:S(2)}) copy-start(f32[256]{0:T(256)} %param.7) | copy-start | bytes 3076
  371.1 291.6 %all-to-all-start.1 = ((bf16[16,256,1408]{1,0,2:T(8,128)(2,1)}), bf16[16,256,1408]{1,0,2:T(8,128)(2,1)}, u32[]{:S(2)}, u32[]{:S(2)}) async-start(bf16[16,256,1408]{1,0,2:T(8,128)(2,1)} %divide_convert_fusion), calls=%async_computation.1 | async-start | bytes 23068672 | tf_op jit(solution)/shard_map/all_to_all | solution.py:22
Sparse Core Ops, SparseCore 0:
  24.0 73.6 all-reduce.2
